TPU v7x, 256 devices: a 2x2x32 block of a 4x8x32 slice. The times are simulated.
256 devices in a mesh: groups: 4 (over y, x), tile: 64 (over z, core).
Axes of the slice: x: 2, y: 2, z: 32, core: 2. Of those that a mesh axis runs over, the one named last changes fastest.
The devices are a block of a 4x8x32 slice.
Arguments:
- self_query: bfloat16 [32768, 4096], P(('groups', 'tile')), parts along dimension 0, may hold values from -110 to 110
- self_key: bfloat16 [32768, 4096], P(('groups', 'tile')), parts along dimension 0, may hold values from -6 to 6
- self_value: bfloat16 [32768, 4096], P(('groups', 'tile')), parts along dimension 0, may hold values from -24 to 24
- cross_query: bfloat16 [32768, 4096], P(('groups', 'tile')), parts along dimension 0, may hold values from -110 to 110
- text_key: bfloat16 [1024, 4096], P(('groups', 'tile')), parts along dimension 0, may hold values from -6 to 6
- text_value: bfloat16 [1024, 4096], P(('groups', 'tile')), parts along dimension 0, may hold values from -24 to 24
- timestep: int32 [1], replicated, may hold values from 0 to 49
- gate_table: bfloat16 [50, 4096], replicated, may hold values from 0.5 to 2
Outputs:
- mixed: bfloat16 [32768, 4096], P(('groups', 'tile')), parts along dimension 0
There are 4 independent parts, one for each index of `groups`. A program takes and returns all parts, laid end to end along the dimension named above; an argument that names none is the same for every part. Nothing has to cross between parts.
All inputs are finite; a program needn't handle non-finite values.
Results may differ from a plain program's by a relative error of at most 0.0032.
Values may be sent and summed in bfloat16 or wider, within the bound.
A program may use at most 64 MiB of HBM per device.

v0:
```python
import math

import jax
import jax.numpy as jnp
from jax import lax
from jax.sharding import PartitionSpec as P

HEADS = 32
RADIUS = 2


def sent_together(arrays, axis, dim, along):
    widths = [a.shape[along] for a in arrays]
    both = jnp.concatenate(arrays, axis=along)
    whole = lax.all_gather(both, axis, axis=dim, tiled=True)
    return tuple(jnp.split(whole, [sum(widths[:k]) for k in range(1, len(widths))], axis=along))


def from_behind(block, axis, distance):
    devices = range(lax.axis_size(axis))
    route = [(i - distance, i) for i in devices if i - distance in devices]
    return lax.ppermute(block, axis, route)


def attend_blocks(queries, key_stack, value_stack, tile_usable):
    row_count, width = queries.shape
    window_span, key_count = (key_stack.shape[0], key_stack.shape[1])
    head_dim = width // HEADS
    head_group = math.gcd(HEADS, 8)
    score_scale = 1.0 / math.sqrt(head_dim)
    usable = tile_usable[None, None, :, None]
    pieces = []
    for block_index in range(HEADS // head_group):
        first = block_index * head_group * head_dim
        last = first + head_group * head_dim
        query_part = queries[:, first:last].reshape(row_count, head_group, head_dim)
        key_part = key_stack[:, :, first:last].reshape(window_span, key_count, head_group, head_dim)
        value_part = value_stack[:, :, first:last].reshape(
            window_span, key_count, head_group, head_dim
        )
        scores = (
            jnp.einsum("qhd,wkhd->hqwk", query_part, key_part, preferred_element_type=jnp.float32)
            * score_scale
        )
        masked = jnp.where(usable, scores, -1e30)
        maxima = jnp.max(masked, axis=(2, 3), keepdims=True)
        weights = jnp.where(usable, jnp.exp(masked - maxima), 0.0)
        totals = jnp.sum(weights, axis=(2, 3))
        rounded = weights.astype(jnp.bfloat16)
        summed = jnp.einsum(
            "hqwk,wkhd->qhd", rounded, value_part, preferred_element_type=jnp.float32
        )
        result = summed / jnp.transpose(totals)[:, :, None]
        pieces.append(result.reshape(row_count, head_group * head_dim))
    return jnp.concatenate(pieces, axis=1)


def shards(
    self_query, self_key, self_value, cross_query, text_key, text_value, timestep, gate_table
):
    radius = RADIUS
    tile_count = lax.axis_size("tile")
    tile_place = lax.axis_index("tile")
    text_keys, text_values = sent_together((text_key, text_value), "tile", 0, 1)
    text_usable = jnp.ones((1,), dtype=bool)
    cross_out = attend_blocks(cross_query, text_keys[None], text_values[None], text_usable)
    own_pair = (self_key, self_value)
    received = {0: own_pair}
    above_pair = own_pair
    below_pair = own_pair
    for distance in range(1, radius + 1):
        above_pair = from_behind((above_pair[0], above_pair[1]), "tile", -1)
        below_pair = from_behind((below_pair[0], below_pair[1]), "tile", 1)
        received[distance] = above_pair
        received[-distance] = below_pair
    ordered = [received[offset] for offset in range(-radius, radius + 1)]
    key_stack = jnp.stack([pair[0] for pair in ordered])
    value_stack = jnp.stack([pair[1] for pair in ordered])
    offsets = jnp.arange(2 * radius + 1, dtype=jnp.int32) - radius
    position = tile_place + offsets
    tile_usable = (position >= 0) & (position < tile_count)
    self_out = attend_blocks(self_query, key_stack, value_stack, tile_usable)
    gate_row = lax.dynamic_slice_in_dim(gate_table, timestep[0], 1, 0).astype(jnp.float32)
    return (gate_row * self_out + cross_out).astype(jnp.bfloat16)


def solution(mesh):
    in_specs = (
        P(("groups", "tile"), None),
        P(("groups", "tile"), None),
        P(("groups", "tile"), None),
        P(("groups", "tile"), None),
        P(("groups", "tile"), None),
        P(("groups", "tile"), None),
        P(),
        P(),
    )
    out_specs = P(("groups", "tile"), None)
    return jax.shard_map(shards, mesh=mesh, in_specs=in_specs, out_specs=out_specs, check_vma=False)
```

profile of v0, /device:TPU:46, one launch (start us, length us, event | category | flops | bytes accessed | tf_op | source)
XLA Modules:
  0.0 220.4 jit_solution(15339642578423144890)
XLA Ops:
  6.6 1.7 copy.134
  8.3 2.9 %collective-permute-start.4 = (bf16[128,4096]{0,1:T(8,128)(2,1)S(1)}, bf16[128,4096]{0,1:T(8,128)(2,1)}, u32[]{:S(2)}, u32[]{:S(2)}) collective-permute-start(bf16[128,4096]{0,1:T(8,128)(2,1)S(1)} %copy.134), channel_id=1, source_target_pairs={{0,1},{1,2},{2,3},{3,4},{4,5},{5,6},{6,7},{7,8},{8,9},{9,10},{10,1... | collective-permute-start | bytes 3145736 | tf_op jit(solution)/shard_map/ppermute | solution.py:22
  11.8 4.3 %collective-permute-start = (bf16[128,4096]{0,1:T(8,128)(2,1)S(1)}, bf16[128,4096]{0,1:T(8,128)(2,1)}, u32[]{:S(2)}, u32[]{:S(2)}) collective-permute-start(bf16[128,4096]{0,1:T(8,128)(2,1)S(1)} %copy.131), channel_id=1, source_target_pairs={{0,1},{1,2},{2,3},{3,4},{4,5},{5,6},{6,7},{7,8},{8,9},{9,10},{10,1... | collective-permute-start | bytes 3145736 | tf_op jit(solution)/shard_map/ppermute | solution.py:22
  19.4 7.8 %collective-permute-start.5 = (bf16[128,4096]{0,1:T(8,128)(2,1)}, bf16[128,4096]{0,1:T(8,128)(2,1)}, u32[]{:S(2)}, u32[]{:S(2)}) collective-permute-start(bf16[128,4096]{0,1:T(8,128)(2,1)} %collective-permute-done.4), channel_id=1, source_target_pairs={{0,1},{1,2},{2,3},{3,4},{4,5},{5,6},{6,7},{7,8},{8,9},{9,10},{10,1... | collective-permute-start | bytes 3145736 | tf_op jit(solution)/shard_map/ppermute | solution.py:22
  30.5 2.0 fusion.86
  32.5 1.8 copy.232
  37.7 3.5 %collective-permute-start.1 = (bf16[128,4096]{0,1:T(8,128)(2,1)}, bf16[128,4096]{0,1:T(8,128)(2,1)S(1)}, u32[]{:S(2)}, u32[]{:S(2)}) collective-permute-start(bf16[128,4096]{0,1:T(8,128)(2,1)} %collective-permute-done), channel_id=1, source_target_pairs={{0,1},{1,2},{2,3},{3,4},{4,5},{5,6},{6,7},{7,8},{8,9},{9,10},{10,1... | collective-permute-start | bytes 3145736 | tf_op jit(solution)/shard_map/ppermute | solution.py:22
  42.5 1.5 collective-permute-start.7
  53.2 1.8 fusion.82
  56.0 3.8 %fusion.10 = (f32[8,128]{1,0:T(8,128)S(1)}, f32[8,128]{1,0:T(8,128)S(1)}, f32[8,128]{1,0:T(8,128)S(1)}, f32[8,128]{1,0:T(8,128)S(1)}, bf16[8,128,5,128]{1,3,2,0:...) fusion(f32[8,5,128,128]{3,2,1,0:T(8,128)S(1)} %get-tuple-element.43, ...), kind=kOutput, calls=%fused_computation.25 | convolution fusion | flops 179564544 | bytes 14704645 | tf_op jit(solution)/shard_map/qhd,wkhd->hqwk/dot_general | solution.py:42
  59.9 2.6 %fusion.14 = (f32[8,128]{1,0:T(8,128)S(1)}, f32[8,128]{1,0:T(8,128)S(1)}, bf16[8,128,5,128]{1,3,2,0:T(8,128)(2,1)}, bf16[8,128,5,128]{1,3,2,0:T(8,128)(2,1)S(1)}) fusion(f32[8,5,128,128]{3,2,1,0:T(8,128)S(1)} %get-tuple-element.44, f32[8,128]{1,0:T(8,128)S(1)} %get-tuple-element.6, pred[5]{0:T(512)(128)(4,1)S(1)} %compare_and_fusion, ...), kind=kLoop, calls=%fused_computation.29 | loop fusion | flops 7862272 | bytes 7880709 | tf_op jit(solution)/shard_map/reduce_sum | solution.py:48
  63.2 2.2 %fusion.57 = f32[128,8,128]{0,2,1:T(8,128)S(1)} fusion(bf16[5,128,8,128]{1,3,2,0:T(8,128)(2,1)} %bitcast.208, bf16[8,128,5,128]{1,3,2,0:T(8,128)(2,1)} %get-tuple-element.25, f32[128,8]{0,1:T(8,128)S(1)} %bitcast.232), kind=kOutput, calls=%fused_computation.84 | convolution fusion | flops 167903232 | bytes 3149824 | tf_op jit(solution)/shard_map/hqwk,wkhd->qhd/dot_general | solution.py:50
  65.6 3.0 %fusion.60 = f32[128,8,128]{0,2,1:T(8,128)} fusion(bf16[5,128,8,128]{1,3,2,0:T(8,128)(2,1)} %bitcast.207, bf16[8,128,5,128]{1,3,2,0:T(8,128)(2,1)} %get-tuple-element.24, f32[128,8]{0,1:T(8,128)S(1)} %bitcast.239), kind=kOutput, calls=%fused_computation.85 | convolution fusion | flops 167903232 | bytes 3149824 | tf_op jit(solution)/shard_map/hqwk,wkhd->qhd/dot_general | solution.py:50
  69.9 2.6 %fusion.63 = f32[128,8,128]{0,2,1:T(8,128)} fusion(bf16[5,128,8,128]{1,3,2,0:T(8,128)(2,1)S(1)} %bitcast.205, bf16[8,128,5,128]{1,3,2,0:T(8,128)(2,1)} %get-tuple-element.23, f32[128,8]{0,1:T(8,128)S(1)} %bitcast.238), kind=kOutput, calls=%fused_computation.86 | convolution fusion | flops 167903232 | bytes 3149824 | tf_op jit(solution)/shard_map/hqwk,wkhd->qhd/dot_general | solution.py:50
  73.7 93.1 %all-gather.3.cloned.1.call-done = bf16[64,4,8192]{2,1,0:T(4,128)(2,1)} async-done(((bf16[1,4,8192]{2,1,0:T(4,128)(2,1)}), bf16[64,4,8192]{2,1,0:T(4,128)(2,1)}) %all-gather.3.cloned.1.call-update) | async-done | bytes 4194320 | tf_op jit(solution)/shard_map/all_gather | solution.py:15
  166.8 6.9 %reshape.224 = bf16[256,8192]{1,0:T(8,128)(2,1)} reshape(bf16[64,4,8192]{2,1,0:T(4,128)(2,1)} %all-gather.3.cloned.1.call-done) | data formatting | bytes 8388608
  173.7 2.7 %slice_bitcast_fusion = (bf16[1,256,4096]{2,1,0:T(8,128)(2,1)S(1)}, bf16[1,256,4096]{2,1,0:T(8,128)(2,1)S(1)}) fusion(bf16[256,8192]{1,0:T(8,128)(2,1)} %reshape.224), kind=kLoop, calls=%fused_computation.20 | loop fusion | bytes 8388608 | tf_op jit(solution)/shard_map/broadcast_in_dim | solution.py:66
  176.5 1.8 fusion.84
  178.2 2.1 copy.175
  181.3 1.5 fusion.88
  185.4 2.0 copy.169
  187.4 2.1 copy.170
  189.5 1.5 fusion.89
  192.3 2.1 copy.183
  194.3 2.0 copy.163
  196.4 2.1 copy.164
  198.4 1.5 fusion.90
  201.3 2.1 copy.182
  203.3 2.0 copy.157
  206.4 1.5 fusion.91
  209.1 2.0 copy.181
  211.2 2.4 %fusion.9 = bf16[128,4096]{1,0:T(8,128)(2,1)} fusion(f32[128,1024]{1,0:T(8,128)S(1)} %copy.156, f32[128,1024]{1,0:T(8,128)S(1)} %copy.155, f32[128,1024]{1,0:T(8,128)S(1)} %copy.154, f32[128,1024]{1,0:T(8,128)S(1)} %copy.153, f32[128,1024]{1,0:T(8,128)S(1)} %copy.184, f32[128,1024]{1,0:T(8,128)S(1)} %copy-done, f32[128,1024]{1,0:T(8,128)} %copy.182, ...), kind=kLoop, calls=%fused_computation.24 | loop fusion | flops 4718592 | bytes 5259264 | tf_op jit(solution)/shard_map/convert_element_type | solution.py:84
  (75 shorter events, 33.1 us)
Async XLA Ops:
  6.5 4.6 %copy-start.1 = (bf16[128,4096]{1,0:T(8,128)(2,1)S(1)}, bf16[128,4096]{1,0:T(8,128)(2,1)}, u32[]{:S(2)}) copy-start(bf16[128,4096]{1,0:T(8,128)(2,1)} %param.10) | copy-start | bytes 3145732
  6.5 12.1 %copy-start.8 = (bf16[4,4096]{1,0:T(4,128)(2,1)S(1)}, bf16[4,4096]{1,0:T(4,128)(2,1)}, u32[]{:S(2)}) copy-start(bf16[4,4096]{1,0:T(4,128)(2,1)} %param.13) | copy-start | bytes 98308
  6.6 12.1 %copy-start.9 = (bf16[4,4096]{1,0:T(4,128)(2,1)S(1)}, bf16[4,4096]{1,0:T(4,128)(2,1)}, u32[]{:S(2)}) copy-start(bf16[4,4096]{1,0:T(4,128)(2,1)} %param.12) | copy-start | bytes 98308
  6.6 160.3 %all-gather.3.cloned.1.call-start = ((), (), s32[]{:S(2)}) async-start(), calls=%async_computation | async-start | bytes 4259840 | tf_op jit(solution)/shard_map/all_gather | solution.py:15
  8.3 11.1 %collective-permute-start.4 = (bf16[128,4096]{0,1:T(8,128)(2,1)S(1)}, bf16[128,4096]{0,1:T(8,128)(2,1)}, u32[]{:S(2)}, u32[]{:S(2)}) collective-permute-start(bf16[128,4096]{0,1:T(8,128)(2,1)S(1)} %copy.134), channel_id=1, source_target_pairs={{0,1},{1,2},{2,3},{3,4},{4,5},{5,6},{6,7},{7,8},{8,9},{9,10},{10,1... | collective-permute-start | bytes 3145736 | tf_op jit(solution)/shard_map/ppermute | solution.py:22
  11.8 25.9 %collective-permute-start = (bf16[128,4096]{0,1:T(8,128)(2,1)S(1)}, bf16[128,4096]{0,1:T(8,128)(2,1)}, u32[]{:S(2)}, u32[]{:S(2)}) collective-permute-start(bf16[128,4096]{0,1:T(8,128)(2,1)S(1)} %copy.131), channel_id=1, source_target_pairs={{0,1},{1,2},{2,3},{3,4},{4,5},{5,6},{6,7},{7,8},{8,9},{9,10},{10,1... | collective-permute-start | bytes 3145736 | tf_op jit(solution)/shard_map/ppermute | solution.py:22
  16.0 25.2 %collective-permute-start.2 = (bf16[128,4096]{0,1:T(8,128)(2,1)S(1)}, bf16[128,4096]{0,1:T(8,128)(2,1)}, u32[]{:S(2)}, u32[]{:S(2)}) collective-permute-start(bf16[128,4096]{0,1:T(8,128)(2,1)S(1)} %copy.131), channel_id=1, source_target_pairs={{1,0},{2,1},{3,2},{4,3},{5,4},{6,5},{7,6},{8,7},{9,8},{10,9},{11,1... | collective-permute-start | bytes 3145736 | tf_op jit(solution)/shard_map/ppermute | solution.py:22
  17.4 25.2 %collective-permute-start.6 = (bf16[128,4096]{0,1:T(8,128)(2,1)S(1)}, bf16[128,4096]{0,1:T(8,128)(2,1)}, u32[]{:S(2)}, u32[]{:S(2)}) collective-permute-start(bf16[128,4096]{0,1:T(8,128)(2,1)S(1)} %copy.134), channel_id=1, source_target_pairs={{1,0},{2,1},{3,2},{4,3},{5,4},{6,5},{7,6},{8,7},{9,8},{10,9},{11,1... | collective-permute-start | bytes 3145736 | tf_op jit(solution)/shard_map/ppermute | solution.py:22
  19.4 24.6 %collective-permute-start.5 = (bf16[128,4096]{0,1:T(8,128)(2,1)}, bf16[128,4096]{0,1:T(8,128)(2,1)}, u32[]{:S(2)}, u32[]{:S(2)}) collective-permute-start(bf16[128,4096]{0,1:T(8,128)(2,1)} %collective-permute-done.4), channel_id=1, source_target_pairs={{0,1},{1,2},{2,3},{3,4},{4,5},{5,6},{6,7},{7,8},{8,9},{9,10},{10,1... | collective-permute-start | bytes 3145736 | tf_op jit(solution)/shard_map/ppermute | solution.py:22
  37.7 11.8 %collective-permute-start.1 = (bf16[128,4096]{0,1:T(8,128)(2,1)}, bf16[128,4096]{0,1:T(8,128)(2,1)S(1)}, u32[]{:S(2)}, u32[]{:S(2)}) collective-permute-start(bf16[128,4096]{0,1:T(8,128)(2,1)} %collective-permute-done), channel_id=1, source_target_pairs={{0,1},{1,2},{2,3},{3,4},{4,5},{5,6},{6,7},{7,8},{8,9},{9,10},{10,1... | collective-permute-start | bytes 3145736 | tf_op jit(solution)/shard_map/ppermute | solution.py:22
  41.2 11.8 %collective-permute-start.3 = (bf16[128,4096]{0,1:T(8,128)(2,1)}, bf16[128,4096]{0,1:T(8,128)(2,1)S(1)}, u32[]{:S(2)}, u32[]{:S(2)}) collective-permute-start(bf16[128,4096]{0,1:T(8,128)(2,1)} %collective-permute-done.2), channel_id=1, source_target_pairs={{1,0},{2,1},{3,2},{4,3},{5,4},{6,5},{7,6},{8,7},{9,8},{10,9},{11,1... | collective-permute-start | bytes 3145736 | tf_op jit(solution)/shard_map/ppermute | solution.py:22
  42.5 5.7 %collective-permute-start.7 = (bf16[128,4096]{0,1:T(8,128)(2,1)}, bf16[128,4096]{0,1:T(8,128)(2,1)S(1)}, u32[]{:S(2)}, u32[]{:S(2)}) collective-permute-start(bf16[128,4096]{0,1:T(8,128)(2,1)} %collective-permute-done.6), channel_id=1, source_target_pairs={{1,0},{2,1},{3,2},{4,3},{5,4},{6,5},{7,6},{8,7},{9,8},{10,9},{11,1... | collective-permute-start | bytes 3145736 | tf_op jit(solution)/shard_map/ppermute | solution.py:22
  53.1 1.9 copy-start.7
  55.0 1.0 copy-start.6
  181.3 1.7 copy-start.3
  189.5 1.7 copy-start.4
  198.4 1.7 copy-start.5
  206.4 1.6 copy-start.2
  208.0 3.2 %copy-start = (f32[128,1024]{1,0:T(8,128)S(1)}, f32[128,1024]{1,0:T(8,128)}, u32[]{:S(2)}) copy-start(f32[128,1024]{1,0:T(8,128)} %copy.183) | copy-start | bytes 1572868
Sparse Core Ops, SparseCore 0:
  19.5 147.2 all-gather.2
where the time goes:
time: 224 us; the launch traced here: 220 us
  waiting for transfers between devices  93.2 us (42%)
  local copies, waits for them, and re-layouts  56.9 us (25%)
  matrix products  24.9 us (11%)
  starting transfers between devices  23.8 us (11%)
  between operations  14.5 us (6%)
  other arithmetic  7.18 us (3%)
    all_gather x1, waiting for transfers between devices, sent_together(): whole = lax.all_gather(both, axis, axis=dim, tiled=True)  93.1 us
    ppermute x8, starting transfers between devices, from_behind(): return lax.ppermute(block, axis, route)  23.8 us
    unnamed x39, local copies, waits for them, and re-layouts  22.1 us
    dot_general x8, matrix products, attend_blocks(): jnp.einsum('hqwk,wkhd->qhd', rounded, value_part, preferred_element_type=...  12.8 us
    dot_general x8, matrix products, attend_blocks(): jnp.einsum('qhd,wkhd->hqwk', query_part, key_part, preferred_element_type...  12 us
    reshape x8, local copies, waits for them, and re-layouts, attend_blocks(): pieces.append(result.reshape(row_count, head_group * head_dim))  10.2 us
    slice x5, local copies, waits for them, and re-layouts, attend_blocks(): value_stack[:, :, first:last]  10 us
    slice x6, local copies, waits for them, and re-layouts, attend_blocks(): key_stack[:, :, first:last]  8.36 us
  transfers between devices with their start and end apart: 9, of which 1 were waited for; matrix products, arithmetic and copies ran while one was open for 18% of the time, Pallas kernels for 0%

commit v1 on v0

v1 whole, which is shorter than its diff:
```python
import functools
import math

import jax
import jax.numpy as jnp
from jax import lax
from jax.experimental import pallas as pl
from jax.experimental.pallas import tpu as pltpu
from jax.sharding import PartitionSpec as P

HEADS = 32
RADIUS = 2
SPAN = 2 * RADIUS + 1
OWN = RADIUS
STEP_NUM, STEP_DEN = 3, 2
RECV_LAG, ATTEND_LAG = 2, 1
NEG = -1e30


def softmax_parts(scores, scale):
    top = jnp.max(scores, axis=1, keepdims=True)
    weights = jnp.exp2((scores - top) * (scale * math.log2(math.e)))
    return weights.astype(jnp.bfloat16), jnp.sum(weights, axis=1, keepdims=True)


def dot(a, b, contract_b):
    return lax.dot_general(a, b, (((1,), (contract_b,)), ((), ())), preferred_element_type=jnp.float32)


def kernel(
    tiles,
    step_ref, self_query, self_key, self_value, cross_query, text_key, text_value, gate_table,
    mixed,
    win, text, query_s, query_c, gates, gate, bias, acc, result,
    own_sem, load_sem,
    up_recv, down_recv, pair_recv, pass_recv, text_recv, text_pair_recv,
    text_sent, send_sem, out_sem,
):
    rows, width = query_s.shape
    dim = width // HEADS
    text_rows = text_key.shape[0]
    scale = 1.0 / math.sqrt(dim)
    chips = tiles // 2
    hops_up = chips // 2
    hops_down = chips - 1 - hops_up

    me = lax.axis_index("tile")
    core = lax.rem(me, 2)
    chip = lax.div(me, 2)
    above = lax.rem(me + 2, tiles)
    below = lax.rem(me + tiles - 2, tiles)
    partner = me + 1 - 2 * core
    has_below = chip > 0
    has_above = chip < chips - 1
    pair_slot = 1 + 2 * core
    pass_src = 4 - 4 * core
    pass_slot = 3 - 2 * core
    sends_pass = jnp.logical_or(jnp.logical_and(core == 1, has_below), jnp.logical_and(core == 0, has_above))
    gets_pass = jnp.logical_or(jnp.logical_and(core == 0, has_below), jnp.logical_and(core == 1, has_above))

    def remote(src, dst, which, recv, target):
        return pltpu.make_async_remote_copy(
            src_ref=src, dst_ref=dst, send_sem=send_sem.at[which], recv_sem=recv,
            device_id={"tile": target}, device_id_type=pl.DeviceIdType.MESH,
        )

    def columns(head):
        return pl.ds(pl.multiple_of(head * dim, dim), dim)

    def block(slot):
        return text.at[:, pl.ds(pl.multiple_of(slot * text_rows, text_rows), text_rows)]

    loads = [
        pltpu.make_async_copy(text_key, text.at[0, pl.ds(0, text_rows)], load_sem.at[0]),
        pltpu.make_async_copy(text_value, text.at[1, pl.ds(0, text_rows)], load_sem.at[1]),
        pltpu.make_async_copy(self_query, query_s, load_sem.at[2]),
        pltpu.make_async_copy(gate_table, gates, load_sem.at[3]),
        pltpu.make_async_copy(cross_query, query_c, load_sem.at[4]),
    ]

    def load_head(head):
        for which, source in enumerate((self_key, self_value)):
            pltpu.make_async_copy(source.at[:, columns(head)], win.at[OWN, head, which], own_sem.at[head]).start()

    def load_heads(first, last):
        lax.fori_loop(first, last, lambda head, c: (load_head(head), c)[1], 0)

    loads[0].start()
    loads[1].start()
    load_heads(0, 4)
    loads[2].start()
    load_heads(4, HEADS)
    loads[3].start()
    loads[4].start()

    barrier = pltpu.get_barrier_semaphore()
    for neighbour in (above, below, partner):
        pl.semaphore_signal(barrier, inc=1, device_id={"tile": neighbour}, device_id_type=pl.DeviceIdType.MESH)
    pl.semaphore_wait(barrier, 3)

    def head_copies(head):
        own = win.at[OWN, head]
        return (
            remote(own, win.at[0, head], 0, up_recv.at[head], above),
            remote(own, win.at[SPAN - 1, head], 1, down_recv.at[head], below),
            remote(own, win.at[pair_slot, head], 2, pair_recv.at[head], partner),
        )

    def pass_copy(head):
        return remote(win.at[pass_src, head], win.at[pass_slot, head], 3, pass_recv.at[head], partner)

    def send_head(head, carry):
        pltpu.make_async_copy(win.at[OWN, head], win.at[OWN, head], own_sem.at[head]).wait()
        up, down, pair = head_copies(head)

        @pl.when(has_above)
        def _():
            up.start()

        @pl.when(has_below)
        def _():
            down.start()

        pair.start()
        return carry

    def take_head(head, carry):
        up, down, _ = head_copies(head)

        @pl.when(has_below)
        def _():
            up.wait_recv()

        @pl.when(has_above)
        def _():
            down.wait_recv()

        @pl.when(sends_pass)
        def _():
            pass_copy(head).start()

        return carry

    def self_attend(head, write):
        pair = head_copies(head)[2]
        pair.wait_recv()

        @pl.when(gets_pass)
        def _():
            pass_copy(head).wait_recv()

        query = query_s[:, columns(head)]
        keys = win[:, head, 0].reshape(SPAN * rows, dim)
        values = win[:, head, 1].reshape(SPAN * rows, dim)
        weights, total = softmax_parts(dot(query, keys, 1) + bias[...], scale)
        attended = dot(weights, values, 0) / total
        mix(head, gate[:, columns(head)] * attended, write)

    def cross_attend(head, write):
        query = query_c[:, columns(head)]
        weights, total = softmax_parts(dot(query, text[0, :, columns(head)], 1), scale)
        mix(head, dot(weights, text[1, :, columns(head)], 0) / total, write)

    def out_copy(head):
        return pltpu.make_async_copy(result.at[:, columns(head)], mixed.at[:, columns(head)], out_sem)

    def mix(head, term, write):
        total = acc[:, columns(head)] + term
        acc[:, columns(head)] = total

        @pl.when(write)
        def _():
            result[:, columns(head)] = total.astype(result.dtype)
            out_copy(head).start()

    def text_copy(src, dst, target):
        return pltpu.make_async_remote_copy(
            src_ref=block(src), dst_ref=block(dst), send_sem=text_sent.at[dst], recv_sem=text_recv.at[dst],
            device_id={"tile": target}, device_id_type=pl.DeviceIdType.MESH,
        )

    def text_pair(slot):
        return remote(block(slot), block(chips + slot), 4, text_pair_recv.at[slot], partner)

    def sent_by(step):
        return jnp.minimum((STEP_NUM * (step + 1)) // STEP_DEN, HEADS) if not isinstance(step, int) else (
            min(max((STEP_NUM * (step + 1)) // STEP_DEN, 0), HEADS))

    def ring_step(step, carry):
        up_slot = step
        down_slot = jnp.where(step == 0, 0, hops_up + step)

        @pl.when(step > 0)
        def _():
            text_copy(0, up_slot, above).wait_recv()

        text_copy(up_slot, step + 1, above).start()

        @pl.when(jnp.logical_and(step > 0, step <= hops_down))
        def _():
            text_copy(0, down_slot, below).wait_recv()

        @pl.when(step < hops_down)
        def _():
            text_copy(down_slot, hops_up + step + 1, below).start()

        lax.fori_loop(sent_by(step - 1), sent_by(step), send_head, 0)
        text_pair(up_slot).start()

        @pl.when(jnp.logical_and(step > 0, step <= hops_down))
        def _():
            text_pair(down_slot).start()

        @pl.when(step == 0)
        def _():
            prepare()

        @pl.when(step >= RECV_LAG)
        def _():
            lax.fori_loop(sent_by(step - RECV_LAG - 1), sent_by(step - RECV_LAG), take_head, 0)

        lag = RECV_LAG + ATTEND_LAG

        @pl.when(step >= lag)
        def _():
            lax.fori_loop(sent_by(step - lag - 1), sent_by(step - lag), attend_only, 0)

        return carry

    def attend_only(head, carry):
        self_attend(head, False)
        return carry

    def prepare():
        usable = (has_below, jnp.logical_or(core == 1, has_below), None, jnp.logical_or(core == 0, has_above), has_above)
        for slot in range(SPAN):
            here = pl.ds(slot * rows, rows)
            if usable[slot] is None:
                bias[:, here] = jnp.zeros((1, rows), jnp.float32)
                continue
            bias[:, here] = jnp.full((1, rows), jnp.where(usable[slot], 0.0, NEG), jnp.float32)

            @pl.when(jnp.logical_not(usable[slot]))
            def _(slot=slot):
                def clear(head, c):
                    win[slot, head] = jnp.zeros(win.shape[2:], win.dtype)
                    return c

                lax.fori_loop(0, HEADS, clear, 0)

        def clear_acc(head, c):
            acc[:, columns(head)] = jnp.zeros((rows, dim), jnp.float32)
            return c

        lax.fori_loop(0, HEADS, clear_acc, 0)
        loads[2].wait()
        loads[3].wait()
        loads[4].wait()
        picked = lax.broadcasted_iota(jnp.int32, (gates.shape[0], dim), 0) == step_ref[0]

        def pick(head, c):
            table = gates[:, columns(head)].astype(jnp.float32)
            gate[:, columns(head)] = jnp.sum(jnp.where(picked, table, 0.0), axis=0, keepdims=True)
            return c

        lax.fori_loop(0, HEADS, pick, 0)

    loads[0].wait()
    loads[1].wait()
    lax.fori_loop(0, hops_up, ring_step, 0)

    sent = sent_by(hops_up - 1)
    taken = sent_by(hops_up - 1 - RECV_LAG) if hops_up > RECV_LAG else 0
    attended = sent_by(hops_up - 1 - RECV_LAG - ATTEND_LAG) if hops_up > RECV_LAG + ATTEND_LAG else 0
    lax.fori_loop(sent, HEADS, send_head, 0)
    text_copy(0, hops_up, above).wait_recv()
    text_pair(hops_up).start()
    lax.fori_loop(attended, taken, attend_only, 0)

    def pair_wait(slot, carry):
        text_pair(slot).wait_recv()
        return carry

    steps = HEADS - taken
    each = -(-HEADS // steps)

    def tail_step(i, carry):
        take_head(taken + i, 0)

        @pl.when(i == 0)
        def _():
            lax.fori_loop(0, chips, pair_wait, 0)

        for k in range(each):
            index = i * each + k

            @pl.when(index < HEADS)
            def _(index=index):
                head = lax.rem(taken + index, HEADS)
                cross_attend(head, head < taken)

        @pl.when(i > 0)
        def _():
            self_attend(taken + i - 1, True)

        return carry

    lax.fori_loop(0, steps, tail_step, 0)
    self_attend(HEADS - 1, True)

    @pl.when(has_above)
    def _():
        remote(win.at[OWN], win.at[0], 0, up_recv.at[0], above).wait_send()

    @pl.when(has_below)
    def _():
        remote(win.at[OWN], win.at[SPAN - 1], 1, down_recv.at[0], below).wait_send()

    remote(win.at[OWN], win.at[pair_slot], 2, pair_recv.at[0], partner).wait_send()

    @pl.when(sends_pass)
    def _():
        remote(win.at[pass_src], win.at[pass_slot], 3, pass_recv.at[0], partner).wait_send()

    def text_gone(slot, carry):
        text_copy(0, slot, above).wait_send()
        return carry

    lax.fori_loop(1, chips, text_gone, 0)
    whole = text.at[:, pl.ds(0, chips * text_rows)]
    remote(whole, whole, 4, text_pair_recv.at[0], partner).wait_send()
    pltpu.make_async_copy(result, mixed, out_sem).wait()


def solution(mesh):
    tiles = mesh.shape["tile"]

    def shards(self_query, self_key, self_value, cross_query, text_key, text_value, timestep, gate_table):
        rows, width = self_query.shape
        dim = width // HEADS
        chips = tiles // 2
        text_rows = text_key.shape[0] * tiles
        bf16, f32 = jnp.bfloat16, jnp.float32
        dma = pltpu.SemaphoreType.DMA
        anywhere = pl.BlockSpec(memory_space=pl.ANY)
        return pl.pallas_call(
            functools.partial(kernel, tiles),
            name="window_attention",
            out_shape=jax.ShapeDtypeStruct((rows, width), bf16),
            in_specs=[pl.BlockSpec(memory_space=pltpu.SMEM)] + [anywhere] * 7,
            out_specs=anywhere,
            scratch_shapes=[
                pltpu.VMEM((SPAN, HEADS, 2, rows, dim), bf16),
                pltpu.VMEM((2, text_rows, width), bf16),
                pltpu.VMEM((rows, width), bf16),
                pltpu.VMEM((rows, width), bf16),
                pltpu.VMEM(gate_table.shape, bf16),
                pltpu.VMEM((1, width), f32),
                pltpu.VMEM((1, SPAN * rows), f32),
                pltpu.VMEM((rows, width), f32),
                pltpu.VMEM((rows, width), bf16),
                dma((HEADS,)),
                dma((5,)),
                dma((HEADS,)),
                dma((HEADS,)),
                dma((HEADS,)),
                dma((HEADS,)),
                dma((chips,)),
                dma((chips,)),
                dma((chips,)),
                dma((5,)),
                dma,
            ],
            compiler_params=pltpu.CompilerParams(collective_id=0, has_side_effects=True),
        )(timestep, self_query, self_key, self_value, cross_query, text_key, text_value, gate_table)

    rowwise = P(("groups", "tile"), None)
    return jax.shard_map(
        shards, mesh=mesh, in_specs=(rowwise,) * 6 + (P(), P()), out_specs=rowwise, check_vma=False
    )
```

time: 224 us -> 111 us (0.50)
  Pallas kernels: 0 us -> 107 us
  waiting for transfers between devices: 93.2 us -> 0 us
  local copies, waits for them, and re-layouts: 56.9 us -> 2.29 us
  matrix products: 24.9 us -> 0 us
  starting transfers between devices: 23.8 us -> 0 us
  between operations: 14.5 us -> 0.66 us
  other arithmetic: 7.18 us -> 0 us
    pallas_call x0 -> x1, Pallas kernels: none -> 107 us  [shards(): pl.pallas_call(functools.partial(kernel, tiles), name='window_attention',...]
    all_gather x1 -> x0, waiting for transfers between devices: 93.1 us -> none  [sent_together(): whole = lax.all_gather(both, axis, axis=dim, tiled=True)]
    dot_general x16 -> x0, matrix products: 24.9 us -> none  [the longest x8 12.8 us: attend_blocks(): jnp.einsum('hqwk,wkhd->qhd', rounded, value_part, preferred_element_type=...]
    ppermute x8 -> x0, starting transfers between devices: 23.8 us -> none  [from_behind(): return lax.ppermute(block, axis, route)]
    slice x13 -> x0, local copies, waits for them, and re-layouts: 21.6 us -> none  [the longest x5 10 us: attend_blocks(): value_stack[:, :, first:last]]
    unnamed x39 -> x1, local copies, waits for them, and re-layouts: 22.1 us -> 2.29 us
    reshape x8 -> x0, local copies, waits for them, and re-layouts: 10.2 us -> none  [attend_blocks(): pieces.append(result.reshape(row_count, head_group * head_dim))]
    reduce_sum x5 -> x0, other arithmetic: 3.23 us -> none  [attend_blocks(): totals = jnp.sum(weights, axis=(2, 3))]
  transfers between devices with their start and end apart: 9 -> 0, of which waited for: 1 -> 0; matrix products, arithmetic and copies ran while one was open for 18% -> 0% of each run, Pallas kernels for 0% -> 0%
where the time goes in v1:
time: 111 us; the launch traced here: 110 us
  Pallas kernels  107 us (96%)
  local copies, waits for them, and re-layouts  2.29 us (2%)
    pallas_call x1, Pallas kernels, shards(): pl.pallas_call(functools.partial(kernel, tiles), name='window_attention',...  107 us
    unnamed x1, local copies, waits for them, and re-layouts  2.29 us

profile of v1, /device:TPU:46, one launch (start us, length us, event | category | flops | bytes accessed | tf_op | source)
XLA Modules:
  0.0 109.6 jit_solution(13073543062308637246)
XLA Ops:
  0.7 106.6 %window_attention.1 = bf16[128,4096]{1,0:T(8,128)(2,1)} custom-call(s32[1]{0:T(128)S(6)} %copy.10.step_ref, bf16[128,4096]{1,0:T(8,128)(2,1)} %self_query.1, bf16[128,4096]{1,0:T(8,128)(2,1)} %self_key.1, bf16[128,4096]{1,0:T(8,128)(2,1)} %self_value.1, bf16[128,4096]{1,0:T(8,128)(2,1)} %cross_query.1, bf16[4,4096]{1,0:T(4,128)(2,1)} %text_key.1, ...), custom_call_target="tpu_custom_call" | custom-call | tf_op jit(solution)/shard_map/window_attention/pallas_call | solution.py:346
  107.3 2.3 %copy.11 = bf16[128,4096]{1,0:T(8,128)(2,1)} copy(bf16[128,4096]{1,0:T(8,128)(2,1)} %window_attention.1) | data formatting | bytes 2097152
